TPU v7x, 256 devices: a whole 4x4x8 slice. The times are simulated.
256 devices in a mesh: ep: 16 (over y, x), fsdp: 16 (over z, core).
Axes of the slice: x: 4, y: 4, z: 8, core: 2. Of those that a mesh axis runs over, the one named last changes fastest.
Arguments:
- w_gate: float32 [64, 2048, 1024], P('ep', 'fsdp'), may hold values from -0.1875 to 0.1875
- avg_gate: bfloat16 [64, 2048, 1024], P('ep', 'fsdp'), may hold values from -0.0625 to 0.0625
- w_up: float32 [64, 2048, 1024], P('ep', 'fsdp'), may hold values from -0.1875 to 0.1875
- avg_up: bfloat16 [64, 2048, 1024], P('ep', 'fsdp'), may hold values from -0.0625 to 0.0625
- w_down: float32 [64, 1024, 2048], P('ep', None, 'fsdp'), may hold values from -0.25 to 0.25
- avg_down: bfloat16 [64, 1024, 2048], P('ep', None, 'fsdp'), may hold values from -0.09375 to 0.09375
- router_weight: float32 [2048, 64], P('fsdp', 'ep'), may hold values from -0.125 to 0.125
- router_gain: float32 [2048], P('fsdp'), may hold values from 0.25 to 1.75
Outputs:
- serve_gate: bfloat16 [64, 2048, 1024], P('ep', None, 'fsdp')
- serve_up: bfloat16 [64, 2048, 1024], P('ep', None, 'fsdp')
- serve_down: bfloat16 [64, 1024, 2048], P('ep', 'fsdp')
- scale_gate: float32 [64, 1024], P('ep', 'fsdp')
- scale_up: float32 [64, 1024], P('ep', 'fsdp')
- scale_down: float32 [64, 1024], P('ep', 'fsdp')
- serve_router: bfloat16 [2048, 64], replicated
All inputs are finite; a program needn't handle non-finite values.
Results may differ from a plain program's by a relative error of at most 0.001.
Values may be sent and summed in bfloat16 or wider, within the bound.
A program may use at most 64 MiB of HBM per device.

v0:
```python
import jax
import jax.numpy as jnp
from jax import lax
from jax.sharding import PartitionSpec as P


def sent_to_all(x, axis):
    devices = lax.axis_size(axis)
    return lax.all_to_all(jnp.broadcast_to(x[None], (devices, *x.shape)), axis, 0, 0, tiled=True)


def of_everyone(x, axis):
    return sent_to_all(x, axis).sum(axis=0)


def together(arrays, axis):
    ends = [0]
    for a in arrays:
        ends.append(ends[-1] + a.size)
    running = of_everyone(jnp.concatenate([a.ravel() for a in arrays]), axis)
    return tuple((running[b:e].reshape(a.shape) for a, b, e in zip(arrays, ends, ends[1:])))


def side_by_side(arrays, axis, split_dim, concat_dim, along):
    both = jnp.concatenate(arrays, axis=along)
    filled, at, gathered = (
        lax.all_to_all(both, axis, split_axis=split_dim, concat_axis=concat_dim, tiled=True),
        0,
        [],
    )
    for a in arrays:
        gathered.append(lax.slice_in_dim(filled, at, at + a.shape[along], axis=along))
        at += a.shape[along]
    return tuple(gathered)


def in_order(blocks, dim):
    shape = list(blocks.shape[1:])
    shape[dim] *= blocks.shape[0]
    return jnp.moveaxis(blocks, 0, dim).reshape(shape)


def gather_directly(x, axis, dim):
    blocks = sent_to_all(x, axis)
    return in_order(blocks, dim)


def on_device(w_gate, avg_gate, w_up, avg_up, w_down, avg_down, router_weight, router_gain):
    fresh_gate = w_gate + avg_gate.astype(jnp.float32)
    fresh_up = w_up + avg_up.astype(jnp.float32)
    fresh_down = w_down + avg_down.astype(jnp.float32)
    total_gate, total_up, total_down = together(
        (
            jnp.sum(fresh_gate * fresh_gate, axis=1),
            jnp.sum(fresh_up * fresh_up, axis=1),
            jnp.sum(fresh_down * fresh_down, axis=2),
        ),
        "fsdp",
    )
    scale_gate = jnp.sqrt(total_gate)
    scale_up = jnp.sqrt(total_up)
    scale_down = jnp.sqrt(total_down)
    narrow_gate, narrow_up, narrow_down = (
        (fresh_gate / jnp.expand_dims(scale_gate, 1)).astype(jnp.bfloat16),
        (fresh_up / jnp.expand_dims(scale_up, 1)).astype(jnp.bfloat16),
        (fresh_down / jnp.expand_dims(scale_down, 2)).astype(jnp.bfloat16),
    )
    serve_gate, serve_up = side_by_side((narrow_gate, narrow_up), "fsdp", 2, 1, 0)
    serve_down = lax.all_to_all(narrow_down, "fsdp", split_axis=1, concat_axis=2, tiled=True)
    scale_gate = lax.dynamic_slice_in_dim(
        scale_gate, lax.axis_index("fsdp") * serve_gate.shape[2], serve_gate.shape[2], axis=1
    )
    scale_up = lax.dynamic_slice_in_dim(
        scale_up, lax.axis_index("fsdp") * serve_up.shape[2], serve_up.shape[2], axis=1
    )
    scale_down = lax.dynamic_slice_in_dim(
        scale_down, lax.axis_index("fsdp") * serve_down.shape[1], serve_down.shape[1], axis=1
    )
    part_router = (router_weight * router_gain[:, None]).astype(jnp.bfloat16)
    row_router = gather_directly(part_router, "fsdp", 0)
    serve_router = gather_directly(row_router, "ep", 1)
    return (serve_gate, serve_up, serve_down, scale_gate, scale_up, scale_down, serve_router)


def solution(mesh):
    placed = (
        P("ep", "fsdp", None),
        P("ep", "fsdp", None),
        P("ep", "fsdp", None),
        P("ep", "fsdp", None),
        P("ep", None, "fsdp"),
        P("ep", None, "fsdp"),
        P("fsdp", "ep"),
        P("fsdp"),
    )
    return jax.shard_map(
        on_device,
        mesh=mesh,
        in_specs=placed,
        out_specs=(
            P("ep", None, "fsdp"),
            P("ep", None, "fsdp"),
            P("ep", "fsdp", None),
            P("ep", "fsdp"),
            P("ep", "fsdp"),
            P("ep", "fsdp"),
            P(),
        ),
        check_vma=False,
    )
```

profile of v0, /device:TPU:1, one launch (start us, length us, event | category | flops | bytes accessed | tf_op | source)
XLA Modules:
  0.0 152.4 jit_solution(10923737695649039242)
XLA Ops:
  0.6 0.7 multiply_convert_fusion
  1.3 0.6 broadcast_in_dim.9
  1.9 10.0 %all-to-all-start.3 = ((bf16[16,128,4]{1,2,0:T(4,128)(2,1)}), bf16[16,128,4]{1,2,0:T(4,128)(2,1)S(1)}, u32[]{:S(2)}, u32[]{:S(2)}) async-start(bf16[16,128,4]{1,2,0:T(4,128)(2,1)} %broadcast_in_dim.9), calls=%async_computation.3 | async-start | bytes 32768 | tf_op jit(solution)/shard_map/all_to_all | solution.py:9
  11.9 2.4 %multiply_reduce_fusion.2 = f32[4,1024]{1,0:T(4,128)S(1)} fusion(f32[4,128,1024]{2,1,0:T(8,128)} %param.8, bf16[4,128,1024]{2,1,0:T(8,128)(2,1)} %param.9), kind=kLoop, calls=%fused_computation.8 | loop fusion | flops 2093056 | bytes 3162112 | tf_op jit(solution)/shard_map/reduce_sum | solution.py:54
  14.7 0.4 multiply_reduce_fusion.1
  15.1 0.9 copy-done
  16.3 0.6 multiply_reduce_fusion
  16.9 2.3 %all-to-all-done.3 = bf16[16,128,4]{1,2,0:T(4,128)(2,1)S(1)} async-done(((bf16[16,128,4]{1,2,0:T(4,128)(2,1)}), bf16[16,128,4]{1,2,0:T(4,128)(2,1)S(1)}, u32[]{:S(2)}, u32[]{:S(2)}) %all-to-all-start.3) | async-done | bytes 16416 | tf_op jit(solution)/shard_map/all_to_all | solution.py:9
  19.2 0.6 broadcast_in_dim.8
  19.8 27.6 %all_to_all.49 = f32[16,1,12288]{2,1,0:T(1,128)} all-to-all(f32[16,1,12288]{2,1,0:T(1,128)S(1)} %broadcast_in_dim.8), channel_id=1, replica_groups=mesh['ep'=16,'fsdp'=16] {'fsdp'}, dimensions={0} | all-to-all | bytes 1572864 | tf_op jit(solution)/shard_map/all_to_all | solution.py:9
  47.5 0.8 broadcast_in_dim.11
  48.3 6.8 %all-to-all-start.4 = ((bf16[16,2048,4]{1,2,0:T(4,128)(2,1)}), bf16[16,2048,4]{1,2,0:T(4,128)(2,1)S(1)}, u32[]{:S(2)}, u32[]{:S(2)}) async-start(bf16[16,2048,4]{1,2,0:T(4,128)(2,1)} %broadcast_in_dim.11), calls=%async_computation.4 | async-start | bytes 524288 | tf_op jit(solution)/shard_map/all_to_all | solution.py:9
  55.0 1.6 %reduce_sum.39 = f32[12288]{0:T(1024)S(1)} reduce(f32[16,1,12288]{2,1,0:T(1,128)} %all_to_all.49, f32[]{:T(128)} %constant.5.clone.1), dimensions={0,1}, to_apply=%region_3.0 | reduce | flops 184320 | bytes 835588 | tf_op jit(solution)/shard_map/reduce_sum | solution.py:13
  56.7 0.7 divide_convert_fusion
  57.5 1.8 %copy.115 = bf16[4,1024,128]{2,0,1:T(4,128)(2,1)} copy(bf16[4,1024,128]{2,1,0:T(8,128)(2,1)S(1)} %divide_convert_fusion) | data formatting | bytes 2097152 | tf_op jit(solution)/shard_map/convert_element_type | solution.py:66
  59.3 4.3 %all-to-all-done.4 = bf16[16,2048,4]{1,2,0:T(4,128)(2,1)S(1)} async-done(((bf16[16,2048,4]{1,2,0:T(4,128)(2,1)}), bf16[16,2048,4]{1,2,0:T(4,128)(2,1)S(1)}, u32[]{:S(2)}, u32[]{:S(2)}) %all-to-all-start.4) | async-done | bytes 262176 | tf_op jit(solution)/shard_map/all_to_all | solution.py:9
  63.6 5.1 %all-to-all-start.2 = ((bf16[4,1024,128]{2,0,1:T(4,128)(2,1)}), bf16[4,1024,128]{2,0,1:T(4,128)(2,1)}, u32[]{:S(2)}, u32[]{:S(2)}) async-start(bf16[4,1024,128]{2,0,1:T(4,128)(2,1)} %copy.115), calls=%async_computation.2 | async-start | bytes 2097152 | tf_op jit(solution)/shard_map/all_to_all | solution.py:69
  68.8 0.4 divide_convert_fusion.1
  69.2 1.2 copy-done.3
  70.6 0.4 divide_convert_fusion.2
  71.2 2.9 %copy.111 = bf16[8,128,1024]{1,0,2:T(8,128)(2,1)} copy(bf16[8,128,1024]{2,1,0:T(8,128)(2,1)S(1)} %pad_maximum_fusion) | data formatting | bytes 4194304 | tf_op jit(solution)/shard_map/concatenate | solution.py:25
  74.1 22.7 %all-to-all-done.2 = bf16[4,1024,128]{2,0,1:T(4,128)(2,1)} async-done(((bf16[4,1024,128]{2,0,1:T(4,128)(2,1)}), bf16[4,1024,128]{2,0,1:T(4,128)(2,1)}, u32[]{:S(2)}, u32[]{:S(2)}) %all-to-all-start.2) | async-done | bytes 1048608 | tf_op jit(solution)/shard_map/all_to_all | solution.py:69
  96.9 3.6 %all-to-all-start.1 = ((bf16[8,128,1024]{1,0,2:T(8,128)(2,1)}), bf16[8,128,1024]{1,0,2:T(8,128)(2,1)S(1)}, u32[]{:S(2)}, u32[]{:S(2)}) async-start(bf16[8,128,1024]{1,0,2:T(8,128)(2,1)} %copy.111), calls=%async_computation.1 | async-start | bytes 4194304 | tf_op jit(solution)/shard_map/all_to_all | solution.py:27
  100.5 0.8 reshape.73
  101.3 0.6 constant_dynamic-slice_fusion
  101.9 0.6 constant_dynamic-slice_fusion.1
  102.6 0.6 constant_dynamic-slice_fusion.2
  103.2 1.9 %copy.116 = bf16[4,64,16,128]{3,2,1,0:T(8,128)(2,1)S(1)} copy(bf16[4,64,16,128]{3,0,1,2:T(4,128)(2,1)} %bitcast.4) | data formatting | bytes 2097152 | tf_op jit(solution)/shard_map/all_to_all | solution.py:69
  105.1 1.3 all_to_all.41
  106.4 43.0 %all-to-all-done.1 = bf16[8,128,1024]{1,0,2:T(8,128)(2,1)S(1)} async-done(((bf16[8,128,1024]{1,0,2:T(8,128)(2,1)}), bf16[8,128,1024]{1,0,2:T(8,128)(2,1)S(1)}, u32[]{:S(2)}, u32[]{:S(2)}) %all-to-all-start.1) | async-done | bytes 2097184 | tf_op jit(solution)/shard_map/all_to_all | solution.py:27
  149.9 1.2 copy.134
  151.1 1.2 copy.135
  (24 shorter events, 1.7 us)
Async XLA Ops:
  1.9 17.3 %all-to-all-start.3 = ((bf16[16,128,4]{1,2,0:T(4,128)(2,1)}), bf16[16,128,4]{1,2,0:T(4,128)(2,1)S(1)}, u32[]{:S(2)}, u32[]{:S(2)}) async-start(bf16[16,128,4]{1,2,0:T(4,128)(2,1)} %broadcast_in_dim.9), calls=%async_computation.3 | async-start | bytes 32768 | tf_op jit(solution)/shard_map/all_to_all | solution.py:9
  11.9 2.5 %copy-start.1 = (f32[4,128,1024]{2,1,0:T(8,128)S(1)}, f32[4,128,1024]{2,1,0:T(8,128)}, u32[]{:S(2)}) copy-start(f32[4,128,1024]{2,1,0:T(8,128)} %param.10) | copy-start | bytes 6291460
  11.9 2.8 %copy-start.5 = (bf16[4,128,1024]{2,1,0:T(8,128)(2,1)S(1)}, bf16[4,128,1024]{2,1,0:T(8,128)(2,1)}, u32[]{:S(2)}) copy-start(bf16[4,128,1024]{2,1,0:T(8,128)(2,1)} %param.11) | copy-start | bytes 3145732
  14.3 1.7 %copy-start = (f32[4,1024,128]{2,1,0:T(8,128)S(1)}, f32[4,1024,128]{2,1,0:T(8,128)}, u32[]{:S(2)}) copy-start(f32[4,1024,128]{2,1,0:T(8,128)} %param.12) | copy-start | bytes 6291460
  14.3 1.9 %copy-start.4 = (bf16[4,1024,128]{2,1,0:T(8,128)(2,1)S(1)}, bf16[4,1024,128]{2,1,0:T(8,128)(2,1)}, u32[]{:S(2)}) copy-start(bf16[4,1024,128]{2,1,0:T(8,128)(2,1)} %param.13) | copy-start | bytes 3145732
  48.3 15.3 %all-to-all-start.4 = ((bf16[16,2048,4]{1,2,0:T(4,128)(2,1)}), bf16[16,2048,4]{1,2,0:T(4,128)(2,1)S(1)}, u32[]{:S(2)}, u32[]{:S(2)}) async-start(bf16[16,2048,4]{1,2,0:T(4,128)(2,1)} %broadcast_in_dim.11), calls=%async_computation.4 | async-start | bytes 524288 | tf_op jit(solution)/shard_map/all_to_all | solution.py:9
  57.5 11.3 %copy-start.2 = (f32[4,128,1024]{2,1,0:T(8,128)S(1)}, f32[4,128,1024]{2,1,0:T(8,128)}, u32[]{:S(2)}) copy-start(f32[4,128,1024]{2,1,0:T(8,128)} %param.10) | copy-start | bytes 6291460
  57.5 11.3 %copy-start.6 = (bf16[4,128,1024]{2,1,0:T(8,128)(2,1)S(1)}, bf16[4,128,1024]{2,1,0:T(8,128)(2,1)}, u32[]{:S(2)}) copy-start(bf16[4,128,1024]{2,1,0:T(8,128)(2,1)} %param.11) | copy-start | bytes 3145732
  63.6 33.3 %all-to-all-start.2 = ((bf16[4,1024,128]{2,0,1:T(4,128)(2,1)}), bf16[4,1024,128]{2,0,1:T(4,128)(2,1)}, u32[]{:S(2)}, u32[]{:S(2)}) async-start(bf16[4,1024,128]{2,0,1:T(4,128)(2,1)} %copy.115), calls=%async_computation.2 | async-start | bytes 2097152 | tf_op jit(solution)/shard_map/all_to_all | solution.py:69
  68.8 1.6 %copy-start.3 = (f32[4,128,1024]{2,1,0:T(8,128)S(1)}, f32[4,128,1024]{2,1,0:T(8,128)}, u32[]{:S(2)}) copy-start(f32[4,128,1024]{2,1,0:T(8,128)} %param.8) | copy-start | bytes 6291460
  68.8 1.8 %copy-start.7 = (bf16[4,128,1024]{2,1,0:T(8,128)(2,1)S(1)}, bf16[4,128,1024]{2,1,0:T(8,128)(2,1)}, u32[]{:S(2)}) copy-start(bf16[4,128,1024]{2,1,0:T(8,128)(2,1)} %param.9) | copy-start | bytes 3145732
  96.9 52.5 %all-to-all-start.1 = ((bf16[8,128,1024]{1,0,2:T(8,128)(2,1)}), bf16[8,128,1024]{1,0,2:T(8,128)(2,1)S(1)}, u32[]{:S(2)}, u32[]{:S(2)}) async-start(bf16[8,128,1024]{1,0,2:T(8,128)(2,1)} %copy.111), calls=%async_computation.1 | async-start | bytes 4194304 | tf_op jit(solution)/shard_map/all_to_all | solution.py:27
where the time goes:
time: 153 us; the launch traced here: 152 us
  waiting for transfers between devices  72.4 us (47%)
  blocking collectives  27.6 us (18%)
  starting transfers between devices  25.5 us (17%)
  local copies, waits for them, and re-layouts  18.7 us (12%)
  other arithmetic  7.38 us (5%)
    all_to_all x1, waiting for transfers between devices, side_by_side(): lax.all_to_all(both, axis, split_axis=split_dim, concat_axis=concat_dim,...  43 us
    all_to_all x1, blocking collectives, sent_to_all(): lax.all_to_all(jnp.broadcast_to(x[None], (devices, *x.shape)), axis, 0, 0...  27.6 us
    all_to_all x1, waiting for transfers between devices, on_device(): lax.all_to_all(narrow_down, 'fsdp', split_axis=1, concat_axis=2, tiled=True)  22.7 us
    all_to_all x2, starting transfers between devices, sent_to_all(): lax.all_to_all(jnp.broadcast_to(x[None], (devices, *x.shape)), axis, 0, 0...  16.7 us
    all_to_all x2, waiting for transfers between devices, sent_to_all(): lax.all_to_all(jnp.broadcast_to(x[None], (devices, *x.shape)), axis, 0, 0...  6.68 us
    all_to_all x1, starting transfers between devices, on_device(): lax.all_to_all(narrow_down, 'fsdp', split_axis=1, concat_axis=2, tiled=True)  5.12 us
    all_to_all x1, starting transfers between devices, side_by_side(): lax.all_to_all(both, axis, split_axis=split_dim, concat_axis=concat_dim,...  3.62 us
    unnamed x18, local copies, waits for them, and re-layouts  3.29 us
  transfers between devices with their start and end apart: 4, of which 4 were waited for; matrix products, arithmetic and copies ran while one was open for 11% of the time, Pallas kernels for 0%

commit v1 on v0

v1 whole, which is shorter than its diff:
```python
import jax
import jax.numpy as jnp
from jax import lax
from jax.experimental import pallas as pl
from jax.experimental.pallas import tpu as pltpu
from jax.sharding import PartitionSpec as P

MESH = pl.DeviceIdType.MESH
RING = 8
PEERS = 2 * RING
EACH = 4
UNITS = 3 * EACH
LANES = 128
HALF = 64
FAR_FIRST = (4, 3, -3, 2, -2, 1, -1)


def others(me):
    chip, core = me // 2, me % 2
    found = [2 * chip + 1 - core]
    for step in FAR_FIRST:
        there = lax.rem(chip + step + RING, RING)
        found += [2 * there + core, 2 * there + 1 - core]
    return found


def block(i):
    return pl.ds(pl.multiple_of(i * LANES, LANES), LANES)


def wait_for(ref, sem):
    pltpu.make_async_copy(ref, ref, sem).wait()


def exchange(
    w_gate, avg_gate, w_up, avg_up, w_down, avg_down, router_weight, router_gain,
    out, own_total, router,
    fresh, change, raw, raw_change, weight, gain,
    even, odd, parts, got, total, totals, inverse, ready, rows, columns,
    load_sem, part_send, part_recv, total_send, total_recv,
    send, recv, row_send, row_recv, column_send, column_recv,
):
    me, group = lax.axis_index("fsdp"), lax.axis_index("ep")
    barrier = pltpu.get_barrier_semaphore()

    def greet(i, _):
        pl.semaphore_signal(barrier, inc=1, device_id={"fsdp": lax.rem(me + i, PEERS)}, device_id_type=MESH)
        pl.semaphore_signal(barrier, inc=1, device_id={"ep": lax.rem(group + i, PEERS)}, device_id_type=MESH)
        return 0

    lax.fori_loop(1, PEERS, greet, 0)
    loads = []
    for w, avg, at in ((w_gate, avg_gate, 0), (w_up, avg_up, EACH)):
        for e in range(EACH):
            loads.append((w.at[e], fresh.at[at + e]))
            loads.append((avg.at[e], change.at[at + e]))
    for e in range(EACH):
        loads.append((w_down.at[e], raw.at[e]))
        loads.append((avg_down.at[e], raw_change.at[e]))
    loads += [(router_weight, weight), (router_gain, gain)]
    loads = [pltpu.make_async_copy(a, b, load_sem.at[i]) for i, (a, b) in enumerate(loads)]
    for copy in loads:
        copy.start()

    even[6:8, :] = jnp.zeros((2, even.shape[1]), jnp.float32)
    odd[6:8, :] = jnp.zeros((2, odd.shape[1]), jnp.float32)

    for u in range(UNITS):
        loads[2 * u].wait()
        loads[2 * u + 1].wait()
        sums, row = (even, odd)[u % 2], u // 2
        if u < 2 * EACH:

            def add_up(i, acc):
                at = pl.ds(pl.multiple_of(i * 16, 16), 16)
                x = fresh[u, at, :] + change[u, at, :].astype(jnp.float32)
                fresh[u, at, :] = x
                x = x * x
                return acc + x[:8] + x[8:]

            acc = lax.fori_loop(0, 8, add_up, jnp.zeros((8, 1024), jnp.float32))
            sums[row : row + 1, :] = jnp.sum(acc, axis=0, keepdims=True)
        else:
            e = u - 2 * EACH

            def add_across(b, _):
                x = raw[e, block(b), :] + raw_change[e, block(b), :].astype(jnp.float32)
                x = x.T
                fresh[u, :, block(b)] = x
                sums[row : row + 1, block(b)] = jnp.sum(x * x, axis=0, keepdims=True)
                return 0

            lax.fori_loop(0, 8, add_across, 0)
    loads[-2].wait()
    loads[-1].wait()
    rows[:, block(me)] = (weight[...] * gain[...]).astype(jnp.bfloat16)

    low = lax.broadcasted_iota(jnp.int32, (8, LANES), 1) < HALF
    first = jnp.concatenate([even[0:1, LANES * z : LANES * (z + 1)] for z in range(RING)], axis=0)
    for z in range(RING):
        a, b = even[:, LANES * z : LANES * (z + 1)], odd[:, LANES * z : LANES * (z + 1)]
        parts[2 * z, 0:8, :] = jnp.where(low, a, pltpu.roll(b, HALF, 1))
        parts[2 * z + 1, 0:8, :] = jnp.where(low, pltpu.roll(a, HALF, 1), b)
        parts[2 * z, 8:16, :] = first
        parts[2 * z + 1, 8:16, :] = first
    got[me] = parts[me]

    pl.semaphore_wait(barrier, 2 * (PEERS - 1))
    peers = others(me)

    def push(src, dst, send_sem, recv_sem, where):
        pltpu.make_async_remote_copy(
            src_ref=src, dst_ref=dst, send_sem=send_sem, recv_sem=recv_sem, device_id=where, device_id_type=MESH
        ).start()

    for d in peers:
        push(parts.at[d], got.at[me], part_send, part_recv, {"fsdp": d})
    for d in peers:
        push(rows.at[:, block(me)], rows.at[:, block(me)], row_send, row_recv, {"fsdp": d})

    def normalise(u):
        for z in range(RING):
            x = fresh[u, :, LANES * z : LANES * (z + 1)] * inverse[u, z : z + 1, :]
            x = x.T.astype(jnp.bfloat16)
            ready[u, 2 * z] = x[:HALF]
            ready[u, 2 * z + 1] = x[HALF:]
        out[u, :, block(me)] = ready[u, me]

    def spread(u):
        for d in peers:
            push(ready.at[u, d], out.at[u, :, block(me)], send.at[u], recv.at[u], {"fsdp": d})

    wait_for(got.at[pl.ds(0, PEERS - 1)], part_recv)
    summed = got[0]
    for d in range(1, PEERS):
        summed = summed + got[d]
    total[...] = summed[0:8]
    totals[me] = summed[0:8]
    own_total[...] = summed[0:8]
    inverse[0] = 1.0 / jnp.sqrt(summed[8:16])
    for d in peers:
        push(total, totals.at[me], total_send, total_recv, {"fsdp": d})
    normalise(0)
    spread(0)

    wait_for(rows.at[:, pl.ds(0, LANES * (PEERS - 1))], row_recv)
    columns[group] = rows[...]

    def to_group(i, _):
        push(rows, columns.at[group], column_send, column_recv, {"ep": lax.rem(group + i, PEERS)})
        return 0

    lax.fori_loop(1, PEERS, to_group, 0)

    wait_for(totals.at[pl.ds(0, PEERS - 1)], total_recv)
    for z in range(RING):
        a, b = 1.0 / jnp.sqrt(totals[2 * z]), 1.0 / jnp.sqrt(totals[2 * z + 1])
        c, d = jnp.where(low, a, pltpu.roll(b, HALF, 1)), jnp.where(low, pltpu.roll(a, HALF, 1), b)
        for r in range(UNITS // 2):
            inverse[2 * r, z : z + 1, :] = c[r : r + 1]
            inverse[2 * r + 1, z : z + 1, :] = d[r : r + 1]

    def step(u, _):
        normalise(u)
        spread(u)
        return 0

    lax.fori_loop(1, UNITS, step, 0)

    wait_for(columns.at[pl.ds(0, PEERS - 1)], column_recv)
    for p in range(PEERS):
        router[4 * p : 4 * p + 4, :] = columns[p]

    def arrive(u, _):
        wait_for(out.at[u, :, pl.ds(0, LANES * (PEERS - 1))], recv.at[u])
        wait_for(ready.at[u, pl.ds(0, PEERS - 1)], send.at[u])
        return 0

    lax.fori_loop(0, UNITS, arrive, 0)
    wait_for(parts.at[pl.ds(0, PEERS - 1)], part_send)
    wait_for(totals.at[pl.ds(0, PEERS - 1)], total_send)
    wait_for(rows.at[:, pl.ds(0, LANES * (PEERS - 1))], row_send)
    wait_for(columns.at[pl.ds(0, PEERS - 1)], column_send)


def settle(out, own_total, router, gate, up, down, scale_gate, scale_up, scale_down, serve_router, sem):
    copies = [
        pltpu.make_async_copy(out.at[pl.ds(EACH * i, EACH)], to, sem.at[i]) for i, to in enumerate((gate, up, down))
    ]
    copies.append(pltpu.make_async_copy(router, serve_router, sem.at[3]))
    for copy in copies:
        copy.start()
    for i, scale in enumerate((scale_gate, scale_up, scale_down)):
        for e in range(EACH):
            r, h = divmod(EACH * i + e, 2)
            scale[e : e + 1, :] = jnp.sqrt(own_total[r : r + 1, HALF * h : HALF * (h + 1)])
    for copy in copies:
        copy.wait()


def on_device(w_gate, avg_gate, w_up, avg_up, w_down, avg_down, router_weight, router_gain):
    f32, bf16 = jnp.float32, jnp.bfloat16
    hbm, vmem = pl.BlockSpec(memory_space=pltpu.HBM), pl.BlockSpec(memory_space=pltpu.VMEM)
    dma = pltpu.SemaphoreType.DMA
    held = pl.pallas_call(
        exchange,
        out_shape=(
            pltpu.VMEM((UNITS, HALF, 2048), bf16),
            pltpu.VMEM((8, LANES), f32),
            pltpu.VMEM((HALF, 2048), bf16),
        ),
        in_specs=[hbm] * 8,
        out_specs=(vmem,) * 3,
        scratch_shapes=[
            pltpu.VMEM((UNITS, LANES, 1024), f32),
            pltpu.VMEM((2 * EACH, LANES, 1024), bf16),
            pltpu.VMEM((EACH, 1024, LANES), f32),
            pltpu.VMEM((EACH, 1024, LANES), bf16),
            pltpu.VMEM((4, LANES), f32),
            pltpu.VMEM((1, LANES), f32),
            pltpu.VMEM((8, 1024), f32),
            pltpu.VMEM((8, 1024), f32),
            pltpu.VMEM((PEERS, 16, LANES), f32),
            pltpu.VMEM((PEERS, 16, LANES), f32),
            pltpu.VMEM((8, LANES), f32),
            pltpu.VMEM((PEERS, 8, LANES), f32),
            pltpu.VMEM((UNITS, RING, LANES), f32),
            pltpu.VMEM((UNITS, PEERS, HALF, LANES), bf16),
            pltpu.VMEM((4, 2048), bf16),
            pltpu.VMEM((PEERS, 4, 2048), bf16),
            dma((2 * UNITS + 2,)),
            dma(()), dma(()), dma(()), dma(()),
            dma((UNITS,)), dma((UNITS,)),
            dma(()), dma(()), dma(()), dma(()),
        ],
        compiler_params=pltpu.CompilerParams(
            collective_id=0, has_side_effects=True, vmem_limit_bytes=60 << 20
        ),
        name="exchange",
    )(w_gate, avg_gate, w_up, avg_up, w_down, avg_down, router_weight.T, router_gain[None, :])
    served = jax.ShapeDtypeStruct((EACH, HALF, 2048), bf16)
    scale = jax.ShapeDtypeStruct((EACH, HALF), f32)
    gate, up, down, scale_gate, scale_up, scale_down, router = pl.pallas_call(
        settle,
        out_shape=(served, served, served, scale, scale, scale, jax.ShapeDtypeStruct((HALF, 2048), bf16)),
        in_specs=[vmem] * 3,
        out_specs=(hbm, hbm, hbm, vmem, vmem, vmem, hbm),
        scratch_shapes=[dma((4,))],
        compiler_params=pltpu.CompilerParams(vmem_limit_bytes=8 << 20),
        name="settle",
    )(*held)
    turned = (0, 2, 1)
    return (
        gate.transpose(turned), up.transpose(turned), down, scale_gate, scale_up, scale_down, router.T
    )


def solution(mesh):
    placed = (
        P("ep", "fsdp", None),
        P("ep", "fsdp", None),
        P("ep", "fsdp", None),
        P("ep", "fsdp", None),
        P("ep", None, "fsdp"),
        P("ep", None, "fsdp"),
        P("fsdp", "ep"),
        P("fsdp"),
    )
    return jax.shard_map(
        on_device,
        mesh=mesh,
        in_specs=placed,
        out_specs=(
            P("ep", None, "fsdp"),
            P("ep", None, "fsdp"),
            P("ep", "fsdp", None),
            P("ep", "fsdp"),
            P("ep", "fsdp"),
            P("ep", "fsdp"),
            P(),
        ),
        check_vma=False,
    )
```

time: 153 us -> 92.1 us (0.60)
  Pallas kernels: 0 us -> 91.3 us
  waiting for transfers between devices: 72.4 us -> 0 us
  blocking collectives: 27.6 us -> 0 us
  starting transfers between devices: 25.5 us -> 0 us
  local copies, waits for them, and re-layouts: 18.7 us -> 0 us
  other arithmetic: 7.38 us -> 0 us
    pallas_call x0 -> x2, Pallas kernels: none -> 91.3 us  [the longest x1 89 us: on_device(): pl.pallas_call(exchange, out_shape=(pltpu.VMEM((UNITS, HALF, 2048), bf16)...]
    all_to_all x4 -> x0, waiting for transfers between devices: 72.4 us -> none  [the longest x1 43 us: side_by_side(): lax.all_to_all(both, axis, split_axis=split_dim, concat_axis=concat_dim,...]
    all_to_all x1 -> x0, blocking collectives: 27.6 us -> none  [sent_to_all(): lax.all_to_all(jnp.broadcast_to(x[None], (devices, *x.shape)), axis, 0, 0...]
    all_to_all x4 -> x0, starting transfers between devices: 25.5 us -> none  [the longest x2 16.7 us: sent_to_all(): lax.all_to_all(jnp.broadcast_to(x[None], (devices, *x.shape)), axis, 0, 0...]
    reduce_sum x4 -> x0, other arithmetic: 4.99 us -> none  [the longest x1 2.36 us: on_device(): jnp.sum(fresh_gate * fresh_gate, axis=1)]
    all_to_all x3 -> x0, local copies, waits for them, and re-layouts: 3.45 us -> none  [the longest x2 3.18 us: on_device(): lax.all_to_all(narrow_down, 'fsdp', split_axis=1, concat_axis=2, tiled=True)]
    unnamed x18 -> x0, local copies, waits for them, and re-layouts: 3.29 us -> none
    concatenate x1 -> x0, local copies, waits for them, and re-layouts: 2.9 us -> none  [side_by_side(): both = jnp.concatenate(arrays, axis=along)]
  transfers between devices with their start and end apart: 4 -> 0, of which waited for: 4 -> 0; matrix products, arithmetic and copies ran while one was open for 11% -> 0% of each run, Pallas kernels for 0% -> 0%
where the time goes in v1:
time: 92.1 us; the launch traced here: 92 us
  Pallas kernels  91.3 us (99%)
    pallas_call x1, Pallas kernels, on_device(): pl.pallas_call(exchange, out_shape=(pltpu.VMEM((UNITS, HALF, 2048), bf16)...  89 us
    pallas_call x1, Pallas kernels, on_device(): pl.pallas_call(settle, out_shape=(served, served, served, scale, scale, s...  2.36 us

profile of v1, /device:TPU:1, one launch (start us, length us, event | category | flops | bytes accessed | tf_op | source)
XLA Modules:
  0.0 92.0 jit_solution(1387072110180832815)
XLA Ops:
  0.6 89.0 %exchange.1 = (bf16[12,64,2048]{2,1,0:T(8,128)(2,1)S(1)}, f32[8,128]{1,0:T(8,128)S(1)}, bf16[64,2048]{1,0:T(8,128)(2,1)S(1)}) custom-call(f32[4,128,1024]{2,1,0:T(8,128)} %w_gate.1, bf16[4,128,1024]{2,1,0:T(8,128)(2,1)} %avg_gate.1, f32[4,128,1024]{2,1,0:T(8,128)} %w_up.1, bf16[4,128,1024]{2,1,0:T(8,128)(2,1)} %avg_up.1, f32[4,1024,128]{2,1,0:T(8,128)} %w_down.1, ...), custom_call_target="tpu_custom_call" | custom-call | tf_op jit(solution)/shard_map/exchange/pallas_call | solution.py:205
  89.6 2.4 %settle.1 = (bf16[4,64,2048]{2,1,0:T(8,128)(2,1)}, bf16[4,64,2048]{2,1,0:T(8,128)(2,1)}, bf16[4,64,2048]{2,1,0:T(8,128)(2,1)}, f32[4,64]{1,0:T(4,128)}, f32[4,64...) custom-call(bf16[12,64,2048]{2,1,0:T(8,128)(2,1)S(1)} %get-tuple-element.17.out, ...), custom_call_target="tpu_custom_call" | custom-call | tf_op jit(solution)/shard_map/settle/pallas_call | solution.py:243

commit v2 on v1

--- a/solution.py
+++ b/solution.py
@@ -8,20 +8,23 @@
 MESH = pl.DeviceIdType.MESH
 RING = 8
 PEERS = 2 * RING
+AHEAD = (2, 1)
+SHIFT = 6
 EACH = 4
 UNITS = 3 * EACH
 LANES = 128
 HALF = 64
+IN_ORDER = tuple(range(2 * EACH, UNITS)) + tuple(range(2 * EACH))
 FAR_FIRST = (4, 3, -3, 2, -2, 1, -1)
 
 
 def others(me):
     chip, core = me // 2, me % 2
-    found = [2 * chip + 1 - core]
+    found = []
     for step in FAR_FIRST:
         there = lax.rem(chip + step + RING, RING)
         found += [2 * there + core, 2 * there + 1 - core]
-    return found
+    return found + [2 * chip + 1 - core]
 
 
 def block(i):
@@ -43,12 +46,13 @@
     me, group = lax.axis_index("fsdp"), lax.axis_index("ep")
     barrier = pltpu.get_barrier_semaphore()
 
-    def greet(i, _):
-        pl.semaphore_signal(barrier, inc=1, device_id={"fsdp": lax.rem(me + i, PEERS)}, device_id_type=MESH)
-        pl.semaphore_signal(barrier, inc=1, device_id={"ep": lax.rem(group + i, PEERS)}, device_id_type=MESH)
-        return 0
-
-    lax.fori_loop(1, PEERS, greet, 0)
+    peers = others(me)
+
+    def greet(where):
+        pl.semaphore_signal(barrier, inc=1, device_id=where, device_id_type=MESH)
+
+    for d in peers:
+        greet({"fsdp": d})
     loads = []
     for w, avg, at in ((w_gate, avg_gate, 0), (w_up, avg_up, EACH)):
         for e in range(EACH):
@@ -59,13 +63,15 @@
         loads.append((avg_down.at[e], raw_change.at[e]))
     loads += [(router_weight, weight), (router_gain, gain)]
     loads = [pltpu.make_async_copy(a, b, load_sem.at[i]) for i, (a, b) in enumerate(loads)]
-    for copy in loads:
+    for copy in loads[-2:] + [loads[2 * u + i] for u in IN_ORDER for i in range(2)]:
         copy.start()
+    for i in range(1, PEERS):
+        greet({"ep": lax.rem(group + i, PEERS)})
 
     even[6:8, :] = jnp.zeros((2, even.shape[1]), jnp.float32)
     odd[6:8, :] = jnp.zeros((2, odd.shape[1]), jnp.float32)
 
-    for u in range(UNITS):
+    for u in IN_ORDER:
         loads[2 * u].wait()
         loads[2 * u + 1].wait()
         sums, row = (even, odd)[u % 2], u // 2
@@ -78,7 +84,7 @@
                 x = x * x
                 return acc + x[:8] + x[8:]
 
-            acc = lax.fori_loop(0, 8, add_up, jnp.zeros((8, 1024), jnp.float32))
+            acc = lax.fori_loop(0, 8, add_up, jnp.zeros((8, 1024), jnp.float32), unroll=True)
             sums[row : row + 1, :] = jnp.sum(acc, axis=0, keepdims=True)
         else:
             e = u - 2 * EACH
@@ -90,7 +96,7 @@
                 sums[row : row + 1, block(b)] = jnp.sum(x * x, axis=0, keepdims=True)
                 return 0
 
-            lax.fori_loop(0, 8, add_across, 0)
+            lax.fori_loop(0, 8, add_across, 0, unroll=True)
     loads[-2].wait()
     loads[-1].wait()
     rows[:, block(me)] = (weight[...] * gain[...]).astype(jnp.bfloat16)
@@ -106,7 +112,6 @@
     got[me] = parts[me]
 
     pl.semaphore_wait(barrier, 2 * (PEERS - 1))
-    peers = others(me)
 
     def push(src, dst, send_sem, recv_sem, where):
         pltpu.make_async_remote_copy(
@@ -126,9 +131,12 @@
             ready[u, 2 * z + 1] = x[HALF:]
         out[u, :, block(me)] = ready[u, me]
 
+    def to_peer(u, d):
+        push(ready.at[u, d], out.at[u, :, block(me)], send.at[u], recv.at[u], {"fsdp": d})
+
     def spread(u):
         for d in peers:
-            push(ready.at[u, d], out.at[u, :, block(me)], send.at[u], recv.at[u], {"fsdp": d})
+            to_peer(u, d)
 
     wait_for(got.at[pl.ds(0, PEERS - 1)], part_recv)
     summed = got[0]
@@ -165,7 +173,29 @@
         spread(u)
         return 0
 
-    lax.fori_loop(1, UNITS, step, 0)
+    def lead(d):
+        return sum((d < 2 * chips).astype(jnp.int32) for chips in AHEAD)
+
+    def spread_ahead(u, opens):
+        for d in peers:
+            if opens:
+                to_peer(u, d)
+                for i in range(1, len(AHEAD) + 1):
+                    pl.when(lead(d) >= i)(lambda d=d, i=i: to_peer(u + i, d))
+            else:
+                unit = u + lead(d)
+                pl.when(unit < UNITS)(lambda unit=unit, d=d: to_peer(unit, d))
+
+    def step_ahead(u, _):
+        pl.when(u + len(AHEAD) < UNITS)(lambda: normalise(u + len(AHEAD)))
+        spread_ahead(u, False)
+        return 0
+
+    lax.fori_loop(1, SHIFT, step, 0)
+    for i in range(len(AHEAD) + 1):
+        normalise(SHIFT + i)
+    spread_ahead(SHIFT, True)
+    lax.fori_loop(SHIFT + 1, UNITS, step_ahead, 0)
 
     wait_for(columns.at[pl.ds(0, PEERS - 1)], column_recv)
     for p in range(PEERS):
@@ -183,17 +213,21 @@
     wait_for(columns.at[pl.ds(0, PEERS - 1)], column_send)
 
 
-def settle(out, own_total, router, gate, up, down, scale_gate, scale_up, scale_down, serve_router, sem):
-    copies = [
-        pltpu.make_async_copy(out.at[pl.ds(EACH * i, EACH)], to, sem.at[i]) for i, to in enumerate((gate, up, down))
-    ]
-    copies.append(pltpu.make_async_copy(router, serve_router, sem.at[3]))
-    for copy in copies:
+def settle(
+    out, own_total, router, gate, up, down, scale_gate, scale_up, scale_down, serve_router, a, b, c, sem
+):
+    copies = [(out.at[pl.ds(EACH * i, EACH)], to) for i, to in enumerate((gate, up, down))]
+    copies.append((router, serve_router))
+    copies += [(a, scale_gate), (b, scale_up), (c, scale_down)]
+    copies = [pltpu.make_async_copy(x, y, sem.at[i]) for i, (x, y) in enumerate(copies)]
+    for copy in copies[:4]:
         copy.start()
-    for i, scale in enumerate((scale_gate, scale_up, scale_down)):
+    for i, scale in enumerate((a, b, c)):
         for e in range(EACH):
             r, h = divmod(EACH * i + e, 2)
             scale[e : e + 1, :] = jnp.sqrt(own_total[r : r + 1, HALF * h : HALF * (h + 1)])
+    for copy in copies[4:]:
+        copy.start()
     for copy in copies:
         copy.wait()
 
@@ -244,8 +278,8 @@
         settle,
         out_shape=(served, served, served, scale, scale, scale, jax.ShapeDtypeStruct((HALF, 2048), bf16)),
         in_specs=[vmem] * 3,
-        out_specs=(hbm, hbm, hbm, vmem, vmem, vmem, hbm),
-        scratch_shapes=[dma((4,))],
+        out_specs=(hbm,) * 7,
+        scratch_shapes=[pltpu.VMEM((EACH, HALF), f32)] * 3 + [dma((7,))],
         compiler_params=pltpu.CompilerParams(vmem_limit_bytes=8 << 20),
         name="settle",
     )(*held)

time: 92.1 us -> 88.2 us (0.958); the launches traced: 92 us -> 87 us
  Pallas kernels: 91.3 us -> 86.4 us
    pallas_call x1, Pallas kernels: 89 us -> 84.6 us  [on_device(): pl.pallas_call(exchange, out_shape=(pltpu.VMEM((UNITS, HALF, 2048), bf16)...]
where the time goes in v2:
time: 88.2 us; the launch traced here: 87 us
  Pallas kernels  86.4 us (98%)
    pallas_call x1, Pallas kernels, on_device(): pl.pallas_call(exchange, out_shape=(pltpu.VMEM((UNITS, HALF, 2048), bf16)...  84.6 us
    pallas_call x1, Pallas kernels, on_device(): pl.pallas_call(settle, out_shape=(served, served, served, scale, scale, s...  1.81 us

profile of v2, /device:TPU:1, one launch (start us, length us, event | category | flops | bytes accessed | tf_op | source)
XLA Modules:
  0.0 87.0 jit_solution(2864416911972106098)
XLA Ops:
  0.6 84.6 %exchange.1 = (bf16[12,64,2048]{2,1,0:T(8,128)(2,1)S(1)}, f32[8,128]{1,0:T(8,128)S(1)}, bf16[64,2048]{1,0:T(8,128)(2,1)S(1)}) custom-call(f32[4,128,1024]{2,1,0:T(8,128)} %w_gate.1, bf16[4,128,1024]{2,1,0:T(8,128)(2,1)} %avg_gate.1, f32[4,128,1024]{2,1,0:T(8,128)} %w_up.1, bf16[4,128,1024]{2,1,0:T(8,128)(2,1)} %avg_up.1, f32[4,1024,128]{2,1,0:T(8,128)} %w_down.1, ...), custom_call_target="tpu_custom_call" | custom-call | tf_op jit(solution)/shard_map/exchange/pallas_call | solution.py:239
  85.2 1.8 %settle.1 = (bf16[4,64,2048]{2,1,0:T(8,128)(2,1)}, bf16[4,64,2048]{2,1,0:T(8,128)(2,1)}, bf16[4,64,2048]{2,1,0:T(8,128)(2,1)}, f32[4,64]{1,0:T(4,128)}, f32[4,64...) custom-call(bf16[12,64,2048]{2,1,0:T(8,128)(2,1)S(1)} %get-tuple-element.17.out, ...), custom_call_target="tpu_custom_call" | custom-call | tf_op jit(solution)/shard_map/settle/pallas_call | solution.py:277

commit v3 on v2

--- a/solution.py
+++ b/solution.py
@@ -9,12 +9,15 @@
 RING = 8
 PEERS = 2 * RING
 AHEAD = (2, 1)
-SHIFT = 6
+SHIFT = 9
 EACH = 4
 UNITS = 3 * EACH
 LANES = 128
 HALF = 64
-IN_ORDER = tuple(range(2 * EACH, UNITS)) + tuple(range(2 * EACH))
+PAIRS = UNITS // 2
+SOON = 3
+IN_ORDER = tuple(range(2 * SOON)) + tuple(range(2 * EACH, UNITS)) + tuple(range(2 * SOON, 2 * EACH))
+BEFORE_BARRIER = 8
 FAR_FIRST = (4, 3, -3, 2, -2, 1, -1)
 
 
@@ -39,8 +42,9 @@
     w_gate, avg_gate, w_up, avg_up, w_down, avg_down, router_weight, router_gain,
     out, own_total, router,
     fresh, change, raw, raw_change, weight, gain,
-    even, odd, parts, got, total, totals, inverse, ready, rows, columns,
+    even, odd, parts, got, total, totals, late_parts, late_got, late_total, late_totals, inverse, ready, rows, columns,
     load_sem, part_send, part_recv, total_send, total_recv,
+    late_part_send, late_part_recv, late_total_send, late_total_recv,
     send, recv, row_send, row_recv, column_send, column_recv,
 ):
     me, group = lax.axis_index("fsdp"), lax.axis_index("ep")
@@ -68,10 +72,34 @@
     for i in range(1, PEERS):
         greet({"ep": lax.rem(group + i, PEERS)})
 
-    even[6:8, :] = jnp.zeros((2, even.shape[1]), jnp.float32)
-    odd[6:8, :] = jnp.zeros((2, odd.shape[1]), jnp.float32)
-
-    for u in IN_ORDER:
+    def push(src, dst, send_sem, recv_sem, where, priority=0):
+        pltpu.make_async_remote_copy(
+            src_ref=src, dst_ref=dst, send_sem=send_sem, recv_sem=recv_sem, device_id=where, device_id_type=MESH
+        ).start(priority=priority)
+
+    low = lax.broadcasted_iota(jnp.int32, (SOON, LANES), 1) < HALF
+
+    def split(rows, to):
+        for z in range(RING):
+            a, b = even[rows, LANES * z : LANES * (z + 1)], odd[rows, LANES * z : LANES * (z + 1)]
+            to[2 * z, 0:SOON, :] = jnp.where(low, a, pltpu.roll(b, HALF, 1))
+            to[2 * z + 1, 0:SOON, :] = jnp.where(low, pltpu.roll(a, HALF, 1), b)
+
+    for done, u in enumerate(IN_ORDER):
+        if done == 1:
+            loads[-2].wait()
+            loads[-1].wait()
+            rows[:, block(me)] = (weight[...] * gain[...]).astype(jnp.bfloat16)
+        if done == 2 * SOON:
+            split(slice(0, SOON), parts)
+            first = jnp.concatenate([even[0:1, LANES * z : LANES * (z + 1)] for z in range(RING)], axis=0)
+            for d in range(PEERS):
+                parts[d, SOON : SOON + RING, :] = first
+            got[me] = parts[me]
+        if done == BEFORE_BARRIER:
+            pl.semaphore_wait(barrier, 2 * (PEERS - 1))
+            for d in peers:
+                push(parts.at[d], got.at[me], part_send, part_recv, {"fsdp": d})
         loads[2 * u].wait()
         loads[2 * u + 1].wait()
         sums, row = (even, odd)[u % 2], u // 2
@@ -97,29 +125,10 @@
                 return 0
 
             lax.fori_loop(0, 8, add_across, 0, unroll=True)
-    loads[-2].wait()
-    loads[-1].wait()
-    rows[:, block(me)] = (weight[...] * gain[...]).astype(jnp.bfloat16)
-
-    low = lax.broadcasted_iota(jnp.int32, (8, LANES), 1) < HALF
-    first = jnp.concatenate([even[0:1, LANES * z : LANES * (z + 1)] for z in range(RING)], axis=0)
-    for z in range(RING):
-        a, b = even[:, LANES * z : LANES * (z + 1)], odd[:, LANES * z : LANES * (z + 1)]
-        parts[2 * z, 0:8, :] = jnp.where(low, a, pltpu.roll(b, HALF, 1))
-        parts[2 * z + 1, 0:8, :] = jnp.where(low, pltpu.roll(a, HALF, 1), b)
-        parts[2 * z, 8:16, :] = first
-        parts[2 * z + 1, 8:16, :] = first
-    got[me] = parts[me]
-
-    pl.semaphore_wait(barrier, 2 * (PEERS - 1))
-
-    def push(src, dst, send_sem, recv_sem, where):
-        pltpu.make_async_remote_copy(
-            src_ref=src, dst_ref=dst, send_sem=send_sem, recv_sem=recv_sem, device_id=where, device_id_type=MESH
-        ).start()
-
-    for d in peers:
-        push(parts.at[d], got.at[me], part_send, part_recv, {"fsdp": d})
+    split(slice(SOON, PAIRS), late_parts)
+    late_got[me] = late_parts[me]
+    for d in peers:
+        push(late_parts.at[d], late_got.at[me], late_part_send, late_part_recv, {"fsdp": d})
     for d in peers:
         push(rows.at[:, block(me)], rows.at[:, block(me)], row_send, row_recv, {"fsdp": d})
 
@@ -138,38 +147,43 @@
         for d in peers:
             to_peer(u, d)
 
+    def sum_of(each):
+        summed = each[0]
+        for d in range(1, PEERS):
+            summed = summed + each[d]
+        return summed
+
+    def invert(each, row):
+        for z in range(RING):
+            a, b = 1.0 / jnp.sqrt(each[2 * z]), 1.0 / jnp.sqrt(each[2 * z + 1])
+            c, d = jnp.where(low, a, pltpu.roll(b, HALF, 1)), jnp.where(low, pltpu.roll(a, HALF, 1), b)
+            for r in range(SOON):
+                inverse[2 * (row + r), z : z + 1, :] = c[r : r + 1]
+                inverse[2 * (row + r) + 1, z : z + 1, :] = d[r : r + 1]
+
     wait_for(got.at[pl.ds(0, PEERS - 1)], part_recv)
-    summed = got[0]
-    for d in range(1, PEERS):
-        summed = summed + got[d]
-    total[...] = summed[0:8]
-    totals[me] = summed[0:8]
-    own_total[...] = summed[0:8]
-    inverse[0] = 1.0 / jnp.sqrt(summed[8:16])
+    summed = sum_of(got)
+    total[...] = summed[:SOON]
+    totals[me] = summed[:SOON]
+    own_total[0:SOON, :] = summed[:SOON]
+    inverse[0] = 1.0 / jnp.sqrt(summed[SOON:])
     for d in peers:
         push(total, totals.at[me], total_send, total_recv, {"fsdp": d})
     normalise(0)
     spread(0)
 
-    wait_for(rows.at[:, pl.ds(0, LANES * (PEERS - 1))], row_recv)
-    columns[group] = rows[...]
-
-    def to_group(i, _):
-        push(rows, columns.at[group], column_send, column_recv, {"ep": lax.rem(group + i, PEERS)})
-        return 0
-
-    lax.fori_loop(1, PEERS, to_group, 0)
+    wait_for(late_got.at[pl.ds(0, PEERS - 1)], late_part_recv)
+    late_total[...] = sum_of(late_got)
+    late_totals[me] = late_total[...]
+    own_total[SOON:PAIRS, :] = late_total[...]
+    for d in peers:
+        push(late_total, late_totals.at[me], late_total_send, late_total_recv, {"fsdp": d})
 
     wait_for(totals.at[pl.ds(0, PEERS - 1)], total_recv)
-    for z in range(RING):
-        a, b = 1.0 / jnp.sqrt(totals[2 * z]), 1.0 / jnp.sqrt(totals[2 * z + 1])
-        c, d = jnp.where(low, a, pltpu.roll(b, HALF, 1)), jnp.where(low, pltpu.roll(a, HALF, 1), b)
-        for r in range(UNITS // 2):
-            inverse[2 * r, z : z + 1, :] = c[r : r + 1]
-            inverse[2 * r + 1, z : z + 1, :] = d[r : r + 1]
+    invert(totals, 0)
 
     def step(u, _):
-        normalise(u)
+        normalise(u + 1)
         spread(u)
         return 0
 
@@ -191,11 +205,26 @@
         spread_ahead(u, False)
         return 0
 
-    lax.fori_loop(1, SHIFT, step, 0)
-    for i in range(len(AHEAD) + 1):
+    normalise(1)
+    lax.fori_loop(1, 2 * SOON - 1, step, 0)
+    spread(2 * SOON - 1)
+    wait_for(late_totals.at[pl.ds(0, PEERS - 1)], late_total_recv)
+    invert(late_totals, SOON)
+    normalise(2 * SOON)
+    lax.fori_loop(2 * SOON, SHIFT, step, 0)
+    for i in range(1, len(AHEAD) + 1):
         normalise(SHIFT + i)
     spread_ahead(SHIFT, True)
     lax.fori_loop(SHIFT + 1, UNITS, step_ahead, 0)
+
+    wait_for(rows.at[:, pl.ds(0, LANES * (PEERS - 1))], row_recv)
+    columns[group] = rows[...]
+
+    def to_group(i, _):
+        push(rows, columns.at[group], column_send, column_recv, {"ep": lax.rem(group + i, PEERS)})
+        return 0
+
+    lax.fori_loop(1, PEERS, to_group, 0)
 
     wait_for(columns.at[pl.ds(0, PEERS - 1)], column_recv)
     for p in range(PEERS):
@@ -209,6 +238,8 @@
     lax.fori_loop(0, UNITS, arrive, 0)
     wait_for(parts.at[pl.ds(0, PEERS - 1)], part_send)
     wait_for(totals.at[pl.ds(0, PEERS - 1)], total_send)
+    wait_for(late_parts.at[pl.ds(0, PEERS - 1)], late_part_send)
+    wait_for(late_totals.at[pl.ds(0, PEERS - 1)], late_total_send)
     wait_for(rows.at[:, pl.ds(0, LANES * (PEERS - 1))], row_send)
     wait_for(columns.at[pl.ds(0, PEERS - 1)], column_send)
 
@@ -240,7 +271,7 @@
         exchange,
         out_shape=(
             pltpu.VMEM((UNITS, HALF, 2048), bf16),
-            pltpu.VMEM((8, LANES), f32),
+            pltpu.VMEM((PAIRS, LANES), f32),
             pltpu.VMEM((HALF, 2048), bf16),
         ),
         in_specs=[hbm] * 8,
@@ -254,16 +285,20 @@
             pltpu.VMEM((1, LANES), f32),
             pltpu.VMEM((8, 1024), f32),
             pltpu.VMEM((8, 1024), f32),
-            pltpu.VMEM((PEERS, 16, LANES), f32),
-            pltpu.VMEM((PEERS, 16, LANES), f32),
-            pltpu.VMEM((8, LANES), f32),
-            pltpu.VMEM((PEERS, 8, LANES), f32),
+            pltpu.VMEM((PEERS, SOON + RING, LANES), f32),
+            pltpu.VMEM((PEERS, SOON + RING, LANES), f32),
+            pltpu.VMEM((SOON, LANES), f32),
+            pltpu.VMEM((PEERS, SOON, LANES), f32),
+            pltpu.VMEM((PEERS, PAIRS - SOON, LANES), f32),
+            pltpu.VMEM((PEERS, PAIRS - SOON, LANES), f32),
+            pltpu.VMEM((PAIRS - SOON, LANES), f32),
+            pltpu.VMEM((PEERS, PAIRS - SOON, LANES), f32),
             pltpu.VMEM((UNITS, RING, LANES), f32),
             pltpu.VMEM((UNITS, PEERS, HALF, LANES), bf16),
             pltpu.VMEM((4, 2048), bf16),
             pltpu.VMEM((PEERS, 4, 2048), bf16),
             dma((2 * UNITS + 2,)),
-            dma(()), dma(()), dma(()), dma(()),
+            dma(()), dma(()), dma(()), dma(()), dma(()), dma(()), dma(()), dma(()),
             dma((UNITS,)), dma((UNITS,)),
             dma(()), dma(()), dma(()), dma(()),
         ],

time: 88.2 us -> 87.5 us (level)
  no operation moved by 1% of the time
where the time goes in v3:
time: 87.5 us; the launch traced here: 86.2 us
  Pallas kernels  85.6 us (98%)
    pallas_call x1, Pallas kernels, on_device(): pl.pallas_call(exchange, out_shape=(pltpu.VMEM((UNITS, HALF, 2048), bf16)...  83.8 us
    pallas_call x1, Pallas kernels, on_device(): pl.pallas_call(settle, out_shape=(served, served, served, scale, scale, s...  1.81 us

profile of v3, /device:TPU:1, one launch (start us, length us, event | category | flops | bytes accessed | tf_op | source)
XLA Modules:
  0.0 86.2 jit_solution(6605711333755054653)
XLA Ops:
  0.6 83.8 %exchange.1 = (bf16[12,64,2048]{2,1,0:T(8,128)(2,1)S(1)}, f32[6,128]{1,0:T(8,128)S(1)}, bf16[64,2048]{1,0:T(8,128)(2,1)S(1)}) custom-call(f32[4,128,1024]{2,1,0:T(8,128)} %w_gate.1, bf16[4,128,1024]{2,1,0:T(8,128)(2,1)} %avg_gate.1, f32[4,128,1024]{2,1,0:T(8,128)} %w_up.1, bf16[4,128,1024]{2,1,0:T(8,128)(2,1)} %avg_up.1, f32[4,1024,128]{2,1,0:T(8,128)} %w_down.1, ...), custom_call_target="tpu_custom_call" | custom-call | tf_op jit(solution)/shard_map/exchange/pallas_call | solution.py:270
  84.4 1.8 %settle.1 = (bf16[4,64,2048]{2,1,0:T(8,128)(2,1)}, bf16[4,64,2048]{2,1,0:T(8,128)(2,1)}, bf16[4,64,2048]{2,1,0:T(8,128)(2,1)}, f32[4,64]{1,0:T(4,128)}, f32[4,64...) custom-call(bf16[12,64,2048]{2,1,0:T(8,128)(2,1)S(1)} %get-tuple-element.17.out, ...), custom_call_target="tpu_custom_call" | custom-call | tf_op jit(solution)/shard_map/settle/pallas_call | solution.py:312

commit v4 on v3

--- a/solution.py
+++ b/solution.py
@@ -8,16 +8,18 @@
 MESH = pl.DeviceIdType.MESH
 RING = 8
 PEERS = 2 * RING
+WIDE = (2, -2)
 AHEAD = (2, 1)
-SHIFT = 9
+SHIFT = 8
 EACH = 4
 UNITS = 3 * EACH
 LANES = 128
 HALF = 64
 PAIRS = UNITS // 2
 SOON = 3
+LAST = UNITS - 1
 IN_ORDER = tuple(range(2 * SOON)) + tuple(range(2 * EACH, UNITS)) + tuple(range(2 * SOON, 2 * EACH))
-BEFORE_BARRIER = 8
+BEFORE_BARRIER = 10
 FAR_FIRST = (4, 3, -3, 2, -2, 1, -1)
 
 
@@ -42,15 +44,16 @@
     w_gate, avg_gate, w_up, avg_up, w_down, avg_down, router_weight, router_gain,
     out, own_total, router,
     fresh, change, raw, raw_change, weight, gain,
-    even, odd, parts, got, total, totals, late_parts, late_got, late_total, late_totals, inverse, ready, rows, columns,
+    even, odd, wide, widened, parts, got, total, totals, late_parts, late_got, late_total, late_totals, inverse, ready, rows, columns,
     load_sem, part_send, part_recv, total_send, total_recv,
     late_part_send, late_part_recv, late_total_send, late_total_recv,
-    send, recv, row_send, row_recv, column_send, column_recv,
+    send, recv, wide_send, wide_recv, row_send, row_recv, column_send, column_recv,
 ):
     me, group = lax.axis_index("fsdp"), lax.axis_index("ep")
     barrier = pltpu.get_barrier_semaphore()
 
     peers = others(me)
+    chip, core = me // 2, me % 2
 
     def greet(where):
         pl.semaphore_signal(barrier, inc=1, device_id=where, device_id_type=MESH)
@@ -97,6 +100,10 @@
                 parts[d, SOON : SOON + RING, :] = first
             got[me] = parts[me]
         if done == BEFORE_BARRIER:
+            for i, step in enumerate(WIDE):
+                x = fresh[LAST, :, block(lax.rem(chip + step + RING, RING))].T
+                wide[2 * i] = x[:HALF]
+                wide[2 * i + 1] = x[HALF:]
             pl.semaphore_wait(barrier, 2 * (PEERS - 1))
             for d in peers:
                 push(parts.at[d], got.at[me], part_send, part_recv, {"fsdp": d})
@@ -129,6 +136,10 @@
     late_got[me] = late_parts[me]
     for d in peers:
         push(late_parts.at[d], late_got.at[me], late_part_send, late_part_recv, {"fsdp": d})
+    for i, step in enumerate(WIDE):
+        for c in range(2):
+            there = 2 * lax.rem(chip + step + RING, RING) + c
+            push(wide.at[2 * i + c], widened.at[2 * i + core], wide_send, wide_recv, {"fsdp": there})
     for d in peers:
         push(rows.at[:, block(me)], rows.at[:, block(me)], row_send, row_recv, {"fsdp": d})
 
@@ -191,14 +202,15 @@
         return sum((d < 2 * chips).astype(jnp.int32) for chips in AHEAD)
 
     def spread_ahead(u, opens):
-        for d in peers:
+        for i, d in enumerate(peers):
+            end = LAST if i < 2 * RING - 2 and FAR_FIRST[i // 2] in WIDE else UNITS
             if opens:
                 to_peer(u, d)
                 for i in range(1, len(AHEAD) + 1):
                     pl.when(lead(d) >= i)(lambda d=d, i=i: to_peer(u + i, d))
             else:
                 unit = u + lead(d)
-                pl.when(unit < UNITS)(lambda unit=unit, d=d: to_peer(unit, d))
+                pl.when(unit < end)(lambda unit=unit, d=d: to_peer(unit, d))
 
     def step_ahead(u, _):
         pl.when(u + len(AHEAD) < UNITS)(lambda: normalise(u + len(AHEAD)))
@@ -235,7 +247,19 @@
         wait_for(ready.at[u, pl.ds(0, PEERS - 1)], send.at[u])
         return 0
 
-    lax.fori_loop(0, UNITS, arrive, 0)
+    by_row = jnp.broadcast_to(1.0 / jnp.sqrt(own_total[LAST // 2 : LAST // 2 + 1, :]), (LANES, LANES)).T
+    by_row = by_row[HALF * (LAST % 2) : HALF * (LAST % 2 + 1)]
+    wait_for(widened, wide_recv)
+    for i, step in enumerate(WIDE):
+        there = lax.rem(chip - step + RING, RING)
+        for c in range(2):
+            out[LAST, :, block(2 * there + c)] = (widened[2 * i + c] * by_row).astype(jnp.bfloat16)
+
+    lax.fori_loop(0, LAST, arrive, 0)
+    narrow = PEERS - 1 - 2 * len(WIDE)
+    wait_for(out.at[LAST, :, pl.ds(0, LANES * narrow)], recv.at[LAST])
+    wait_for(ready.at[LAST, pl.ds(0, narrow)], send.at[LAST])
+    wait_for(wide, wide_send)
     wait_for(parts.at[pl.ds(0, PEERS - 1)], part_send)
     wait_for(totals.at[pl.ds(0, PEERS - 1)], total_send)
     wait_for(late_parts.at[pl.ds(0, PEERS - 1)], late_part_send)
@@ -285,6 +309,8 @@
             pltpu.VMEM((1, LANES), f32),
             pltpu.VMEM((8, 1024), f32),
             pltpu.VMEM((8, 1024), f32),
+            pltpu.VMEM((2 * len(WIDE), HALF, LANES), f32),
+            pltpu.VMEM((2 * len(WIDE), HALF, LANES), f32),
             pltpu.VMEM((PEERS, SOON + RING, LANES), f32),
             pltpu.VMEM((PEERS, SOON + RING, LANES), f32),
             pltpu.VMEM((SOON, LANES), f32),
@@ -299,7 +325,7 @@
             pltpu.VMEM((PEERS, 4, 2048), bf16),
             dma((2 * UNITS + 2,)),
             dma(()), dma(()), dma(()), dma(()), dma(()), dma(()), dma(()), dma(()),
-            dma((UNITS,)), dma((UNITS,)),
+            dma((UNITS,)), dma((UNITS,)), dma(()), dma(()),
             dma(()), dma(()), dma(()), dma(()),
         ],
         compiler_params=pltpu.CompilerParams(

time: 87.5 us -> 87.3 us (level)
  no operation moved by 1% of the time
where the time goes in v4:
time: 87.3 us; the launch traced here: 86.4 us
  Pallas kernels  85.8 us (98%)
    pallas_call x1, Pallas kernels, on_device(): pl.pallas_call(exchange, out_shape=(pltpu.VMEM((UNITS, HALF, 2048), bf16)...  84 us
    pallas_call x1, Pallas kernels, on_device(): pl.pallas_call(settle, out_shape=(served, served, served, scale, scale, s...  1.81 us

profile of v4, /device:TPU:1, one launch (start us, length us, event | category | flops | bytes accessed | tf_op | source)
XLA Modules:
  0.0 86.4 jit_solution(5987369210820843910)
XLA Ops:
  0.6 84.0 %exchange.1 = (bf16[12,64,2048]{2,1,0:T(8,128)(2,1)S(1)}, f32[6,128]{1,0:T(8,128)S(1)}, bf16[64,2048]{1,0:T(8,128)(2,1)S(1)}) custom-call(f32[4,128,1024]{2,1,0:T(8,128)} %w_gate.1, bf16[4,128,1024]{2,1,0:T(8,128)(2,1)} %avg_gate.1, f32[4,128,1024]{2,1,0:T(8,128)} %w_up.1, bf16[4,128,1024]{2,1,0:T(8,128)(2,1)} %avg_up.1, f32[4,1024,128]{2,1,0:T(8,128)} %w_down.1, ...), custom_call_target="tpu_custom_call" | custom-call | tf_op jit(solution)/shard_map/exchange/pallas_call | solution.py:294
  84.6 1.8 %settle.1 = (bf16[4,64,2048]{2,1,0:T(8,128)(2,1)}, bf16[4,64,2048]{2,1,0:T(8,128)(2,1)}, bf16[4,64,2048]{2,1,0:T(8,128)(2,1)}, f32[4,64]{1,0:T(4,128)}, f32[4,64...) custom-call(bf16[12,64,2048]{2,1,0:T(8,128)(2,1)S(1)} %get-tuple-element.17.out, ...), custom_call_target="tpu_custom_call" | custom-call | tf_op jit(solution)/shard_map/settle/pallas_call | solution.py:338
